TPU v7x, 32 devices: a whole 2x2x4 slice. The times are simulated.
32 devices in a mesh: pipe: 2 (over x), tensor: 4 (over y, core), expert: 4 (over z).
Axes of the slice: x: 2, y: 2, z: 4, core: 2. Of those that a mesh axis runs over, the one named last changes fastest.
Arguments:
- tokens: bfloat16 [2, 256, 4096], P(None, 'expert'), may hold values from -6 to 6
- gains: float32 [2, 4096], P('pipe'), may hold values from 0.1 to 1.9
- route_ids: int32 [2, 2, 256, 2], P('pipe', None, 'expert'), may hold values from 0 to 3, all different within a row
- route_weights: float32 [2, 2, 256, 2], P('pipe', None, 'expert'), may hold values from 0.2 to 1
- picks: int32 [2, 2, 4, 64], P('pipe', None, 'expert'), may hold values from 0 to 63, each once within a row
- w_gate: bfloat16 [2, 4, 4096, 1536], P('pipe', 'expert', None, 'tensor'), may hold values from -0.09375 to 0.09375
- w_up: bfloat16 [2, 4, 4096, 1536], P('pipe', 'expert', None, 'tensor'), may hold values from -0.09375 to 0.09375
- w_down: bfloat16 [2, 4, 1536, 4096], P('pipe', 'expert', 'tensor'), may hold values from -0.15625 to 0.15625
Outputs:
- streams: bfloat16 [2, 2, 256, 4096], P('pipe', None, 'expert', 'tensor')
Inputs may be any that keep to these rules, and one draw needn't show every extreme that they name: `route_ids`: each token names 2 different experts; every expert is named by some token. `picks`: for every layer, micro-batch and block of 64 tokens, a permutation of 0 to 63.
All inputs are finite; a program needn't handle non-finite values.
Results may differ from a plain program's by a relative error of at most 0.025.
Values may be sent and summed in bfloat16 or wider, within the bound.
A program may use at most 64 MiB of HBM per device.

v0:
```python
import functools

import jax
import jax.numpy as jnp
from jax import lax
from jax.experimental import pallas as pl
from jax.experimental.pallas import tpu as pltpu
from jax.sharding import PartitionSpec as P

epsilon = 1e-06
MESH = pl.DeviceIdType.MESH
F32 = jnp.float32
BF16 = jnp.bfloat16


def layer_kernel(
    sizes, tokens, gains_in, ids_in, weights_in, picks_in, w_gate, w_up, w_down, out,
    gains, ids, weights, picks, placing, comb, h_in, fresh, send, x, wg, wu, wd, g_acc, u_acc, own, p_send, p_recv,
    y_send, y_recv, z_send, ret,
    s_sem, w_sem, h_loc, h_send, h_recv, d_send, d_recv, f_send, f_recv, c_send, c_recv,
    ps_sem, pr_sem, ys_sem, yr_sem, zs_sem, zr_sem,
):
    micros, n_p, n_t, n_e, pair, rows_ge, width, capacity = sizes
    n_a = n_t // pair
    cut = (n_e + 1) // 2
    halves = [list(range(cut)), list(range(n_e - 1, cut - 1, -1))]
    p = lax.axis_index("pipe")
    r = lax.axis_index("tensor")
    z = lax.axis_index("expert")
    a = lax.div(r, pair)
    c = lax.rem(r, pair)

    def peer_e(d):
        other = z
        for bit in range(n_e.bit_length()):
            one = 1 << bit
            if d & one:
                other = other + one * (1 - 2 * lax.rem(lax.div(z, one), 2))
        return other

    def rank_of(da, dc):
        return lax.rem(a + da, n_a) * pair + lax.rem(c + dc, pair)

    def remote(src, dst, ssem, rsem, where):
        return pltpu.make_async_remote_copy(
            src_ref=src, dst_ref=dst, send_sem=ssem, recv_sem=rsem,
            device_id=where, device_id_type=MESH,
        )

    loads = [
        pltpu.make_async_copy(w_gate.at[0, 0], wg, w_sem.at[0]),
        pltpu.make_async_copy(w_up.at[0, 0], wu, w_sem.at[1]),
        pltpu.make_async_copy(w_down.at[0, 0], wd, w_sem.at[2]),
    ]

    def first_load(m):
        cols = pl.ds(pl.multiple_of(r * width, width), width)
        return pltpu.make_async_copy(tokens.at[m, :, cols], h_in.at[m], h_loc.at[m])

    small = [
        pltpu.make_async_copy(src, dst, s_sem.at[i])
        for i, (src, dst) in enumerate(
            [(picks_in, picks), (ids_in, ids), (weights_in, weights), (gains_in, gains)]
        )
    ]
    for load in small:
        load.start()

    @pl.when(p == 0)
    def _():
        for m in range(micros):
            first_load(m).start()

    for load in loads:
        load.start()

    barrier = pltpu.get_barrier_semaphore()

    def greet(where):
        pl.semaphore_signal(barrier, inc=1, device_id=where, device_id_type=MESH)

    for d in range(1, n_e):
        greet({"expert": peer_e(d)})
    for da in range(1, n_a):
        greet({"tensor": rank_of(da, 0)})
    for dc in range(1, pair):
        greet({"tensor": rank_of(0, dc)})

    @pl.when(p > 0)
    def _():
        greet({"pipe": p - 1})

    @pl.when(p < n_p - 1)
    def _():
        greet({"pipe": p + 1})

    toks = h_in.shape[1]
    quarter = toks // n_t
    down = lax.broadcasted_iota(jnp.int32, (toks, toks), 0)
    across = lax.broadcasted_iota(jnp.int32, (toks, toks), 1)
    same = down == across

    def column(row):
        return jnp.sum(jnp.where(same, row, jnp.zeros_like(row)), axis=1, keepdims=True)

    def row_of(col):
        return jnp.sum(jnp.where(same, col, jnp.zeros_like(col)), axis=0, keepdims=True)

    def slots(m):
        pos = jnp.sum(jnp.where(picks[m] == down, across, 0), axis=1, keepdims=True)
        pos_row = row_of(pos)
        block = lax.div(pos, quarter)
        before = (lax.div(pos_row, quarter) == block) & (pos_row < pos)
        found = []
        for e in range(n_e):
            named = jnp.zeros((1, toks), jnp.int32)
            for k in range(ids.shape[1]):
                named = named + jnp.where(ids[m, k:k + 1] == e, 1, 0)
            slot = jnp.sum(jnp.where(before, named, 0), axis=1, keepdims=True)
            kept = (column(named) > 0) & (slot < capacity)
            found.append(jnp.where(kept, block * capacity + slot, -1))
        return found

    def place(m, targets):
        places = lax.broadcasted_iota(jnp.int32, (rows_ge, toks), 0)
        for e, target in enumerate(targets):
            placing[m, e] = jnp.where(places == row_of(target), 1.0, 0.0).astype(BF16)

    def weigh(m):
        for e, target in enumerate(slots(m)):
            w_row = jnp.zeros((1, toks), F32)
            for k in range(ids.shape[1]):
                w_row = w_row + jnp.where(ids[m, k:k + 1] == e, weights[m, k:k + 1], 0.0)
            spread = lax.broadcasted_iota(jnp.int32, (toks, rows_ge), 1) == target
            w_col = jnp.where(spread, column(w_row), 0.0)
            high = w_col.astype(BF16)
            comb[m, e, :toks] = high
            comb[m, e, toks:] = (w_col - high.astype(F32)).astype(BF16)

    for load in small:
        load.wait()
    place(0, slots(0))

    ends = jnp.where(p > 0, 1, 0) + jnp.where(p < n_p - 1, 1, 0)
    pl.semaphore_wait(barrier, n_e - 1 + n_a - 1 + pair - 1 + ends)

    def relay(m):
        return remote(fresh.at[m], h_in.at[m], h_send.at[m], h_recv.at[m],
                      {"pipe": jnp.minimum(p + 1, n_p - 1)})

    def d_copy(m, d):
        return remote(send.at[m, d], x.at[m, r, z], d_send.at[m, d], d_recv.at[m, d],
                      {"expert": peer_e(d)})

    def f_copy(m, d, da):
        block = x.at[m, r, peer_e(d)]
        return remote(block, block, f_send.at[m, d, da], f_recv.at[m, d, da],
                      {"tensor": rank_of(da, 0)})

    def c_copy(m, d, da):
        block = x.at[m, rank_of(da, 0), peer_e(d)]
        return remote(block, block, c_send.at[m, d, da], c_recv.at[m, d, da],
                      {"tensor": rank_of(0, 1)})

    def p_copy(m, h, da):
        return remote(p_send.at[m, h, da], p_recv.at[m, h, da], ps_sem.at[m, h, da],
                      pr_sem.at[m, h, da], {"tensor": rank_of(0, 1)})

    def y_copy(m, d, da):
        return remote(y_send.at[m, d, da], y_recv.at[m, d, da], ys_sem.at[m, d, da],
                      yr_sem.at[m, d, da], {"tensor": rank_of(da, 0)})

    def z_copy(m, d):
        return remote(z_send.at[m, d], ret.at[m, z], zs_sem.at[m, d], zr_sem.at[m, d],
                      {"expert": peer_e(d)})

    def dispatch(m):
        @pl.when(p == 0)
        def _():
            first_load(m).wait()

        @pl.when(p > 0)
        def _():
            relay(m).wait_recv()

        h = h_in[m]
        for d in halves[0][1:] + halves[1] + [0]:
            block = jnp.dot(placing[m, peer_e(d)], h, preferred_element_type=F32).astype(BF16)
            if d:
                send[m, d] = block
                d_copy(m, d).start()
            else:
                x[m, r, z] = block

    def forward(m, d):
        if d:
            d_copy(m, d).wait_recv()
        for da in range(1, n_a):
            f_copy(m, d, da).start()
        if pair > 1:
            c_copy(m, d, 0).start()

    def pass_on(m, d):
        for da in range(1, n_a):
            f_copy(m, d, da).wait_recv()
            if pair > 1:
                c_copy(m, d, da).start()

    def compute(m, h):
        if m == 0 and h == 0:
            for load in loads:
                load.wait()
        if pair > 1:
            for d in halves[h]:
                for da in range(n_a):
                    c_copy(m, d, da).wait_recv()
        homes = [peer_e(d) for d in halves[h]]

        def rows_of(q):
            return jnp.concatenate([x[m, q, g].astype(F32) for g in homes], axis=0)

        ss = jnp.zeros((len(homes) * rows_ge, 1), F32)
        for q in range(n_t):
            xf = rows_of(q)
            ss = ss + jnp.sum(xf * xf, axis=-1, keepdims=True)
        inv = lax.rsqrt(ss * (1.0 / (n_t * width)) + epsilon)
        for q in range(n_t):
            cols = slice(q * width, (q + 1) * width)
            nq = (rows_of(q) * inv * gains[0:1, cols]).astype(BF16)
            gq = jnp.dot(nq, wg[cols, :], preferred_element_type=F32)
            uq = jnp.dot(nq, wu[cols, :], preferred_element_type=F32)
            if q == 0:
                g_acc[...] = gq
                u_acc[...] = uq
            else:
                g_acc[...] += gq
                u_acc[...] += uq
        gate = g_acc[...]
        hidden = (gate / (1.0 + jnp.exp(-gate)) * u_acc[...]).astype(BF16)
        for dc in list(range(1, pair)) + [0]:
            for da in list(range(1, n_a)) + [0]:
                start = pl.multiple_of(rank_of(da, dc) * width, width)
                part = jnp.dot(hidden, wd[:, pl.ds(start, width)], preferred_element_type=F32)
                if dc:
                    p_send[m, h, da] = part.astype(BF16)
                    p_copy(m, h, da).start()
                else:
                    own[m, h, da] = part.astype(BF16)

    def reduce_pair(m, h):
        for da in list(range(1, n_a)) + [0]:
            if pair > 1:
                p_copy(m, h, da).wait_recv()
            for i, d in reversed(list(enumerate(halves[h]))) if h == 0 else enumerate(halves[h]):
                part = slice(i * rows_ge, (i + 1) * rows_ge)
                total = own[m, h, da, part].astype(F32)
                if pair > 1:
                    total = total + p_recv[m, h, da, part].astype(F32)
                y_send[m, d, da] = total.astype(BF16)
                if da:
                    y_copy(m, d, da).start()

    def reduce_far(m, d):
        total = y_send[m, d, 0].astype(F32)
        for da in range(1, n_a):
            y_copy(m, d, da).wait_recv()
            total = total + y_recv[m, d, da].astype(F32)
        if d:
            z_send[m, d] = total.astype(BF16)
            z_copy(m, d).start()
        else:
            ret[m, z] = total.astype(BF16)

    def combine(m):
        for d in halves[0] + halves[1]:
            e = peer_e(d)
            if d:
                z_copy(m, d).wait_recv()
            both = jnp.dot(comb[m, e], ret[m, e], preferred_element_type=F32)
            g_part = both[:toks] + both[toks:]
            update = g_part if d == 0 else update + g_part
        new = (h_in[m].astype(F32) + update).astype(BF16)
        fresh[m] = new
        out[0, m] = new

        @pl.when(p < n_p - 1)
        def _():
            relay(m).start()

    first, second = halves

    def step(fn, *args):
        return functools.partial(fn, *args)

    def when(test, fn, *args):
        pl.when(test)(functools.partial(fn, *args))

    def head(m):
        steps = [step(forward, m, d) for d in first]
        steps += [step(pass_on, m, d) for d in first[:-1]]
        steps += [step(forward, m, second[0]), step(pass_on, m, first[-1])]
        if m:
            steps += [step(when, p == 0, forward, m, d) for d in second[1:]]
        return steps

    def middle(m):
        steps = [step(compute, m, 0)]
        if m:
            steps += [step(when, p > 0, forward, m, d) for d in second[1:]]
        else:
            steps += [step(forward, m, d) for d in second[1:]]
        steps += [step(pass_on, m, d) for d in second[:-1]]
        steps += [step(reduce_pair, m, 0), step(weigh, m), step(pass_on, m, second[-1])]
        return steps

    def back(m):
        return [step(compute, m, 1), step(reduce_pair, m, 1)]

    def tail(m):
        return [step(reduce_far, m, d) for d in first[1:] + first[:1] + second]

    def both_of(one, two):
        mixed = []
        for i in range(max(len(one), len(two))):
            mixed += one[i:i + 1] + two[i:i + 1]
        return mixed

    dispatch(0)
    head(0)[0]()
    for m in range(1, micros):
        place(m, slots(m))

    @pl.when(p == 0)
    def _():
        for m in range(1, micros):
            dispatch(m)

    def late_dispatch(m):
        @pl.when(p > 0)
        def _():
            dispatch(m)

    plan = head(0)[1:]
    for m in range(micros):
        plan += middle(m)
        if m:
            plan += [step(when, p < n_p - 1, combine, m - 1)]
        plan += back(m)
        if m + 1 < micros:
            plan += [step(late_dispatch, m + 1)]
            plan += both_of(tail(m), head(m + 1))
    plan += tail(micros - 1)
    plan += [step(when, p == n_p - 1, combine, m) for m in range(micros - 1)]
    plan += [step(combine, micros - 1)]
    for go in plan:
        go()

    for m in range(micros):
        for d in range(n_e):
            if d:
                d_copy(m, d).wait_send()
                z_copy(m, d).wait_send()
            for da in range(n_a):
                if da:
                    f_copy(m, d, da).wait_send()
                    y_copy(m, d, da).wait_send()
                if pair > 1:
                    c_copy(m, d, da).wait_send()
        if pair > 1:
            for h in range(len(halves)):
                for da in range(n_a):
                    p_copy(m, h, da).wait_send()

        @pl.when(p < n_p - 1)
        def _():
            relay(m).wait_send()


def local(mesh_shape, tokens, gains, route_ids, route_weights, picks, w_gate, w_up, w_down):
    n_p, n_t, n_e = mesh_shape
    micros, toks, model_width = tokens.shape
    route_count = route_ids.shape[3]
    quarter = toks // n_t
    capacity = 4 * quarter * route_count // (3 * n_e)
    width = model_width // n_t
    pair = 2 if n_t % 2 == 0 else 1
    n_a = n_t // pair
    rows_ge = -(-n_t * capacity // 8) * 8
    cut = (n_e + 1) // 2
    rows = cut * rows_ge
    hidden_width = w_gate.shape[3]

    ids = route_ids[0].transpose(0, 2, 1)
    weights = route_weights[0].transpose(0, 2, 1)
    order = picks[0]

    sizes = (micros, n_p, n_t, n_e, pair, rows_ge, width, capacity)
    dma = pltpu.SemaphoreType.DMA
    vmem = pl.BlockSpec(memory_space=pltpu.VMEM)
    pinned = pl.BlockSpec(memory_space=pl.ANY)
    return pl.pallas_call(
        functools.partial(layer_kernel, sizes),
        out_shape=jax.ShapeDtypeStruct((1, micros, toks, width), BF16),
        in_specs=[pinned] * 8,
        out_specs=vmem,
        scratch_shapes=[
            pltpu.VMEM(gains.shape, F32),
            pltpu.VMEM(ids.shape, jnp.int32),
            pltpu.VMEM(weights.shape, F32),
            pltpu.VMEM(order.shape, jnp.int32),
            pltpu.VMEM((micros, n_e, rows_ge, toks), BF16),
            pltpu.VMEM((micros, n_e, 2 * toks, rows_ge), BF16),
            pltpu.VMEM((micros, toks, width), BF16),
            pltpu.VMEM((micros, toks, width), BF16),
            pltpu.VMEM((micros, n_e, rows_ge, width), BF16),
            pltpu.VMEM((micros, n_t, n_e, rows_ge, width), BF16),
            pltpu.VMEM(w_gate.shape[2:], BF16),
            pltpu.VMEM(w_up.shape[2:], BF16),
            pltpu.VMEM(w_down.shape[2:], BF16),
            pltpu.VMEM((rows, hidden_width), F32),
            pltpu.VMEM((rows, hidden_width), F32),
            pltpu.VMEM((micros, 2, n_a, rows, width), BF16),
            pltpu.VMEM((micros, 2, n_a, rows, width), BF16),
            pltpu.VMEM((micros, 2, n_a, rows, width), BF16),
            pltpu.VMEM((micros, n_e, n_a, rows_ge, width), BF16),
            pltpu.VMEM((micros, n_e, n_a, rows_ge, width), BF16),
            pltpu.VMEM((micros, n_e, rows_ge, width), BF16),
            pltpu.VMEM((micros, n_e, rows_ge, width), BF16),
            dma((4,)), dma((3,)), dma((micros,)), dma((micros,)), dma((micros,)),
            dma((micros, n_e)), dma((micros, n_e)),
            dma((micros, n_e, n_a)), dma((micros, n_e, n_a)),
            dma((micros, n_e, n_a)), dma((micros, n_e, n_a)),
            dma((micros, 2, n_a)), dma((micros, 2, n_a)),
            dma((micros, n_e, n_a)), dma((micros, n_e, n_a)),
            dma((micros, n_e)), dma((micros, n_e)),
        ],
        compiler_params=pltpu.CompilerParams(
            collective_id=0, has_side_effects=True, vmem_limit_bytes=67043328
        ),
    )(tokens, gains, ids, weights, order, w_gate, w_up, w_down)


def solution(mesh):
    mesh_shape = (mesh.shape["pipe"], mesh.shape["tensor"], mesh.shape["expert"])
    return jax.shard_map(
        functools.partial(local, mesh_shape),
        mesh=mesh,
        in_specs=(
            P(None, "expert", None),
            P("pipe", None),
            P("pipe", None, "expert", None),
            P("pipe", None, "expert", None),
            P("pipe", None, "expert", None),
            P("pipe", "expert", None, "tensor"),
            P("pipe", "expert", None, "tensor"),
            P("pipe", "expert", "tensor", None),
        ),
        out_specs=P("pipe", None, "expert", "tensor"),
        check_vma=False,
    )
```

profile of v0, /device:TPU:6, one launch (start us, length us, event | category | flops | bytes accessed | tf_op | source)
XLA Modules:
  0.0 98.5 jit_solution(1438080304672328747)
XLA Ops:
  0.0 96.9 %shard_map.82 = bf16[1,2,64,1024]{3,2,1,0:T(8,128)(2,1)} custom-call(bf16[2,64,4096]{2,1,0:T(8,128)(2,1)} %tokens.1, f32[1,4096]{1,0:T(1,128)} %gains_in.1, s32[2,2,64]{2,1,0:T(2,128)} %bitcast.9, f32[2,2,64]{2,1,0:T(2,128)} %bitcast.10, s32[2,1,64]{2,1,0:T(1,128)} %bitcast.11, bf16[1,1,4096,384]{3,2,1,0:T(8,128)(2,1)} %w_gate.1, ...), custom_call_target="tpu_custom_call" | custom-call | tf_op jit(solution)/shard_map/pallas_call | solution.py:401
  96.9 1.7 %copy.11 = bf16[1,2,64,1024]{3,2,1,0:T(8,128)(2,1)} copy(bf16[1,2,64,1024]{3,2,1,0:T(8,128)(2,1)} %shard_map.82) | data formatting | bytes 524288
where the time goes:
time: 98.7 us; the launch traced here: 98.5 us
  Pallas kernels  96.9 us (98%)
  local copies, waits for them, and re-layouts  1.67 us (2%)
    pallas_call x1, Pallas kernels, local(): pl.pallas_call(functools.partial(layer_kernel, sizes), out_shape=jax.Shap...  96.9 us

commit v1 on v0

v1 whole, which is shorter than its diff:
```python
import functools

import jax
import jax.numpy as jnp
from jax import lax
from jax.experimental import pallas as pl
from jax.experimental.pallas import tpu as pltpu
from jax.sharding import PartitionSpec as P

epsilon = 1e-06
MESH = pl.DeviceIdType.MESH
F32 = jnp.float32
BF16 = jnp.bfloat16


def layer_kernel(
    sizes, tokens, gains_in, ids_in, weights_in, picks_in, w_gate, w_up, w_down, out,
    gains, ids, weights, picks, placing, comb, h_in, fresh, send, x, wg, wu, wd, g_acc, u_acc, own, p_send, p_recv,
    y_send, y_recv, z_send, ret,
    s_sem, w_sem, o_sem, h_loc, out_sem, h_recv, d_recv, f_recv, c_recv, p_sem, y_sem, z_sem,
):
    micros, n_p, n_t, n_e, pair, parts, rows_ge, width, capacity = sizes
    n_a = n_t // pair
    sub = width // parts
    far_first = list(range(n_e - 1, -1, -1))
    halves = [far_first[0::2], far_first[1::2]]
    halves = [half for half in halves if half]
    ks = range(parts)
    ranks = [(da, dc) for da in range(n_a) for dc in range(pair)]
    p = lax.axis_index("pipe")
    r = lax.axis_index("tensor")
    z = lax.axis_index("expert")
    a = lax.div(r, pair)
    c = lax.rem(r, pair)

    def peer_e(d):
        other = z
        for bit in range(n_e.bit_length()):
            one = 1 << bit
            if d & one:
                other = other + one * (1 - 2 * lax.rem(lax.div(z, one), 2))
        return other

    def rank_of(da, dc):
        return lax.rem(a + da, n_a) * pair + lax.rem(c + dc, pair)

    def remote(src, dst, ssem, rsem, where):
        return pltpu.make_async_remote_copy(
            src_ref=src, dst_ref=dst, send_sem=ssem, recv_sem=rsem,
            device_id=where, device_id_type=MESH,
        )

    loads = [
        pltpu.make_async_copy(w_gate.at[0, 0], wg, w_sem.at[0]),
        pltpu.make_async_copy(w_up.at[0, 0], wu, w_sem.at[1]),
        pltpu.make_async_copy(w_down.at[0, 0], wd, w_sem.at[2]),
    ]

    def first_load(m, k):
        cols = pl.ds(pl.multiple_of(r * width + k * sub, sub), sub)
        return pltpu.make_async_copy(tokens.at[m, :, cols], h_in.at[m, k], h_loc.at[m, k])

    def result(m, k):
        return pltpu.make_async_copy(
            fresh.at[m, k], out.at[0, m, :, k * sub:(k + 1) * sub], o_sem.at[m, k]
        )

    small = [
        pltpu.make_async_copy(src, dst, s_sem.at[i])
        for i, (src, dst) in enumerate(
            [(picks_in, picks), (ids_in, ids), (weights_in, weights), (gains_in, gains)]
        )
    ]
    for load in small:
        load.start()

    @pl.when(p == 0)
    def _():
        for m in range(micros):
            for k in ks:
                first_load(m, k).start()

    for load in loads:
        load.start()

    barrier = pltpu.get_barrier_semaphore()

    def greet(where):
        pl.semaphore_signal(barrier, inc=1, device_id=where, device_id_type=MESH)

    for d in range(1, n_e):
        greet({"expert": peer_e(d)})
    for da in range(1, n_a):
        greet({"tensor": rank_of(da, 0)})
    for dc in range(1, pair):
        greet({"tensor": rank_of(0, dc)})

    @pl.when(p > 0)
    def _():
        greet({"pipe": p - 1})

    @pl.when(p < n_p - 1)
    def _():
        greet({"pipe": p + 1})

    toks = h_in.shape[2]
    quarter = toks // n_t
    down = lax.broadcasted_iota(jnp.int32, (toks, toks), 0)
    across = lax.broadcasted_iota(jnp.int32, (toks, toks), 1)
    same = down == across

    def column(row):
        return jnp.sum(jnp.where(same, row, jnp.zeros_like(row)), axis=1, keepdims=True)

    def row_of(col):
        return jnp.sum(jnp.where(same, col, jnp.zeros_like(col)), axis=0, keepdims=True)

    def slots(m):
        pos = jnp.sum(jnp.where(picks[m] == down, across, 0), axis=1, keepdims=True)
        pos_row = row_of(pos)
        block = lax.div(pos, quarter)
        before = (lax.div(pos_row, quarter) == block) & (pos_row < pos)
        found = []
        for e in range(n_e):
            named = jnp.zeros((1, toks), jnp.int32)
            for k in range(ids.shape[1]):
                named = named + jnp.where(ids[m, k:k + 1] == e, 1, 0)
            slot = jnp.sum(jnp.where(before, named, 0), axis=1, keepdims=True)
            kept = (column(named) > 0) & (slot < capacity)
            found.append(jnp.where(kept, block * capacity + slot, -1))
        return found

    def place(m):
        places = lax.broadcasted_iota(jnp.int32, (rows_ge, toks), 0)
        for e, target in enumerate(slots(m)):
            placing[m, e] = jnp.where(places == row_of(target), 1.0, 0.0).astype(BF16)

    def weigh(m):
        for e, target in enumerate(slots(m)):
            w_row = jnp.zeros((1, toks), F32)
            for k in range(ids.shape[1]):
                w_row = w_row + jnp.where(ids[m, k:k + 1] == e, weights[m, k:k + 1], 0.0)
            spread = lax.broadcasted_iota(jnp.int32, (toks, rows_ge), 1) == target
            w_col = jnp.where(spread, column(w_row), 0.0)
            high = w_col.astype(BF16)
            comb[m, e, :toks] = high
            comb[m, e, toks:] = (w_col - high.astype(F32)).astype(BF16)

    for load in small:
        load.wait()
    place(0)

    ends = jnp.where(p > 0, 1, 0) + jnp.where(p < n_p - 1, 1, 0)
    pl.semaphore_wait(barrier, n_e - 1 + n_a - 1 + pair - 1 + ends)

    def relay(m, k):
        return remote(fresh.at[m, k], h_in.at[m, k], out_sem.at[0], h_recv.at[m, k],
                      {"pipe": jnp.minimum(p + 1, n_p - 1)})

    def d_copy(m, d, k):
        return remote(send.at[m, d, k], x.at[m, r, z, k], out_sem.at[1], d_recv.at[m, d - 1, k],
                      {"expert": peer_e(d)})

    def f_copy(m, d, da, k):
        block = x.at[m, r, peer_e(d), k]
        return remote(block, block, out_sem.at[2], f_recv.at[m, d, da - 1, k],
                      {"tensor": rank_of(da, 0)})

    def c_copy(m, d, da, k):
        block = x.at[m, rank_of(da, 0), peer_e(d), k]
        return remote(block, block, out_sem.at[3], c_recv.at[m, half_of(d), da],
                      {"tensor": rank_of(0, 1)})

    def half_of(d):
        return [h for h, half in enumerate(halves) if d in half][0]

    def shared(m, h, da):
        block = x.at[m, 0, 0:len(halves[h])]
        return remote(block, block, out_sem.at[3], c_recv.at[m, h, da], {"tensor": rank_of(0, 1)})

    def p_copy(m, h, da):
        return remote(p_send.at[m, h, da], p_recv.at[m, h, da], out_sem.at[4],
                      p_sem.at[m, h, da], {"tensor": rank_of(0, 1)})

    def y_copy(m, d, da, k):
        return remote(y_send.at[m, da, d, k], y_recv.at[m, da, d, k], out_sem.at[5],
                      y_sem.at[m, d, da - 1, k], {"tensor": rank_of(da, 0)})

    def z_copy(m, d, k):
        return remote(z_send.at[m, k, d], ret.at[m, k, z], out_sem.at[6], z_sem.at[m, k],
                      {"expert": peer_e(d)})

    def returned(m, k):
        block = ret.at[m, k, 1:n_e]
        return remote(block, block, out_sem.at[6], z_sem.at[m, k], {"expert": peer_e(1)})

    def arrive(m, k, first):
        if first:
            first_load(m, k).wait()
        else:
            relay(m, k).wait_recv()

    def dispatch(m, blocks):
        for d, k in blocks:
            block = jnp.dot(placing[m, peer_e(d)], h_in[m, k], preferred_element_type=F32).astype(BF16)
            if d:
                send[m, d, k] = block
            else:
                x[m, r, z, k] = block
        for d, k in blocks:
            if d:
                d_copy(m, d, k).start()

    def forward(m, d):
        for k in ks:
            if d:
                d_copy(m, d, k).wait_recv()
            for da in range(1, n_a):
                f_copy(m, d, da, k).start()
            if pair > 1:
                c_copy(m, d, 0, k).start()

    def pass_on(m, d):
        for k in ks:
            for da in range(1, n_a):
                f_copy(m, d, da, k).wait_recv()
                if pair > 1:
                    c_copy(m, d, da, k).start()

    squares = {}

    def gate(m, h, i):
        da, dc = ranks[i]
        if m == 0 and h == 0 and i == 0:
            loads[0].wait()
            loads[1].wait()
        if dc:
            shared(m, h, da).wait_recv()
        q = rank_of(da, dc)
        gq = uq = None
        ss = squares.get((m, h))
        for k in ks:
            xf = jnp.concatenate([x[m, q, peer_e(d), k].astype(F32) for d in halves[h]], axis=0)
            part = jnp.sum(xf * xf, axis=-1, keepdims=True)
            ss = part if ss is None else ss + part
            start = pl.multiple_of(q * width + k * sub, sub)
            xg = (xf * gains[0:1, pl.ds(start, sub)]).astype(BF16)
            g1 = jnp.dot(xg, wg[pl.ds(start, sub), :], preferred_element_type=F32)
            u1 = jnp.dot(xg, wu[pl.ds(start, sub), :], preferred_element_type=F32)
            gq = g1 if gq is None else gq + g1
            uq = u1 if uq is None else uq + u1
        squares[m, h] = ss
        if i == 0:
            g_acc[...] = gq
            u_acc[...] = uq
        else:
            g_acc[...] += gq
            u_acc[...] += uq

    def finish(m, h):
        if m == 0 and h == 0:
            loads[2].wait()
        inv = lax.rsqrt(squares[m, h] * (1.0 / (n_t * width)) + epsilon)
        g = g_acc[...] * inv
        hidden = (g / (1.0 + jnp.exp(-g)) * (u_acc[...] * inv)).astype(BF16)
        order = list(range(1, n_a)) + [0]
        for dc in list(range(1, pair)) + [0]:
            for da in order:
                for k in ks:
                    start = pl.multiple_of(rank_of(da, dc) * width + k * sub, sub)
                    part = jnp.dot(hidden, wd[:, pl.ds(start, sub)], preferred_element_type=F32)
                    if dc:
                        p_send[m, h, da, k] = part.astype(BF16)
                    else:
                        own[m, h, da, k] = part.astype(BF16)
            if dc:
                for da in order:
                    p_copy(m, h, da).start()

    def reduce_pair(m, h):
        for da in list(range(1, n_a)) + [0]:
            if pair > 1:
                p_copy(m, h, da).wait_recv()
            for i, d in enumerate(halves[h]):
                for k in ks:
                    part = slice(i * rows_ge, (i + 1) * rows_ge)
                    total = own[m, h, da, k, part].astype(F32)
                    if pair > 1:
                        total = total + p_recv[m, h, da, k, part].astype(F32)
                    y_send[m, da, d, k] = total.astype(BF16)
                    if da:
                        y_copy(m, d, da, k).start()

    def reduce_far(m, d):
        for k in ks:
            total = y_send[m, 0, d, k].astype(F32)
            for da in range(1, n_a):
                y_copy(m, d, da, k).wait_recv()
                total = total + y_recv[m, da, d, k].astype(F32)
            if d:
                z_send[m, k, d] = total.astype(BF16)
                z_copy(m, d, k).start()
            else:
                ret[m, k, z] = total.astype(BF16)

    def combine(m):
        for k in ks:
            returned(m, k).wait_recv()
            for d in range(n_e):
                e = peer_e(d)
                both = jnp.dot(comb[m, e], ret[m, k, e], preferred_element_type=F32)
                g_part = both[:toks] + both[toks:]
                update = g_part if d == 0 else update + g_part
            fresh[m, k] = (h_in[m, k].astype(F32) + update).astype(BF16)

            @pl.when(p < n_p - 1)
            def _():
                relay(m, k).start()

            result(m, k).start()

    def step(fn, *args):
        return functools.partial(fn, *args)

    near, rest = halves[0], [d for d in halves[1] if d]
    last = len(ranks)

    def spread(m, first):
        order = near + rest + [0]
        if first:
            steps = [step(arrive, m, k, first) for k in ks]
            return steps + [step(dispatch, m, [(d, k) for d in order for k in ks])]
        steps = []
        for k in ks:
            steps += [step(arrive, m, k, first), step(dispatch, m, [(d, k) for d in order])]
        return steps

    def gates(m, h, low, high):
        return [step(gate, m, h, i) for i in range(low, high)]

    def each(fn, m, blocks):
        return [step(fn, m, d) for d in blocks]

    def plan_for(first):
        plan = []
        if not first:
            plan += [step(place, m) for m in range(1, micros)]
            plan += [step(weigh, m) for m in range(micros)]
        plan += spread(0, first) + [step(forward, 0, 0)]
        if first:
            plan += [step(place, m) for m in range(1, micros)]
        for m in range(micros):
            ahead = first and m
            more = m + 1 < micros
            plan += each(pass_on, m, [0])
            if not ahead:
                plan += each(forward, m, near)
            plan += gates(m, 0, 0, pair)
            if ahead:
                plan += [step(combine, m - 1)]
            plan += each(pass_on, m, near)
            plan += gates(m, 0, pair, last - 1)
            if not ahead:
                plan += each(forward, m, rest)
            if first and m == 0:
                for n in range(1, micros):
                    plan += spread(n, first)
            plan += gates(m, 0, last - 1, last)
            plan += [step(finish, m, 0)]
            plan += gates(m, 1, 0, pair)
            plan += [step(reduce_pair, m, 0)]
            if m and not first:
                plan += [step(combine, m - 1)]
            plan += each(pass_on, m, rest)
            plan += gates(m, 1, pair, last - 1)
            if first:
                plan += [step(weigh, m)]
            plan += gates(m, 1, last - 1, last)
            plan += [step(finish, m, 1)]
            plan += each(reduce_far, m, near[:1])
            plan += [step(reduce_pair, m, 1)]
            if more:
                if first:
                    plan += each(forward, m + 1, [0] + near + rest)
                else:
                    plan += spread(m + 1, first)
                    plan += each(forward, m + 1, [0])
            plan += each(reduce_far, m, near[1:] + rest + [0])
        plan += [step(combine, micros - 1)]
        return plan

    def follow(first):
        squares.clear()
        for go in plan_for(first):
            go()

    @pl.when(p == 0)
    def _():
        follow(True)

    @pl.when(p > 0)
    def _():
        follow(False)

    def sent(block, i):
        remote(block, block, out_sem.at[i], out_sem.at[i], {"expert": peer_e(1)}).wait_send()

    sent(send.at[:, 1:n_e], 1)
    if n_a > 1:
        sent(x.at[:, 0:n_a - 1], 2)
        sent(y_send.at[:, 1:n_a], 5)
    if pair > 1:
        sent(x.at[:, 0:n_a], 3)
        sent(p_send, 4)
    sent(z_send.at[:, :, 1:n_e], 6)
    for m in range(micros):
        for k in ks:
            result(m, k).wait()

    @pl.when(p < n_p - 1)
    def _():
        sent(fresh, 0)


def local(mesh_shape, tokens, gains, route_ids, route_weights, picks, w_gate, w_up, w_down):
    n_p, n_t, n_e = mesh_shape
    micros, toks, model_width = tokens.shape
    route_count = route_ids.shape[3]
    quarter = toks // n_t
    capacity = 4 * quarter * route_count // (3 * n_e)
    width = model_width // n_t
    pair = 2 if n_t % 2 == 0 else 1
    parts = 2 if width % 256 == 0 else 1
    sub = width // parts
    n_a = n_t // pair
    rows_ge = -(-n_t * capacity // 8) * 8
    rows = (n_e + 1) // 2 * rows_ge
    hidden_width = w_gate.shape[3]

    ids = route_ids[0].transpose(0, 2, 1)
    weights = route_weights[0].transpose(0, 2, 1)
    order = picks[0]

    sizes = (micros, n_p, n_t, n_e, pair, parts, rows_ge, width, capacity)
    dma = pltpu.SemaphoreType.DMA
    pinned = pl.BlockSpec(memory_space=pl.ANY)
    return pl.pallas_call(
        functools.partial(layer_kernel, sizes),
        out_shape=jax.ShapeDtypeStruct((1, micros, toks, width), BF16),
        in_specs=[pinned] * 8,
        out_specs=pinned,
        scratch_shapes=[
            pltpu.VMEM(gains.shape, F32),
            pltpu.VMEM(ids.shape, jnp.int32),
            pltpu.VMEM(weights.shape, F32),
            pltpu.VMEM(order.shape, jnp.int32),
            pltpu.VMEM((micros, n_e, rows_ge, toks), BF16),
            pltpu.VMEM((micros, n_e, 2 * toks, rows_ge), BF16),
            pltpu.VMEM((micros, parts, toks, sub), BF16),
            pltpu.VMEM((micros, parts, toks, sub), BF16),
            pltpu.VMEM((micros, n_e, parts, rows_ge, sub), BF16),
            pltpu.VMEM((micros, n_t, n_e, parts, rows_ge, sub), BF16),
            pltpu.VMEM(w_gate.shape[2:], BF16),
            pltpu.VMEM(w_up.shape[2:], BF16),
            pltpu.VMEM(w_down.shape[2:], BF16),
            pltpu.VMEM((rows, hidden_width), F32),
            pltpu.VMEM((rows, hidden_width), F32),
            pltpu.VMEM((micros, 2, n_a, parts, rows, sub), BF16),
            pltpu.VMEM((micros, 2, n_a, parts, rows, sub), BF16),
            pltpu.VMEM((micros, 2, n_a, parts, rows, sub), BF16),
            pltpu.VMEM((micros, n_a, n_e, parts, rows_ge, sub), BF16),
            pltpu.VMEM((micros, n_a, n_e, parts, rows_ge, sub), BF16),
            pltpu.VMEM((micros, parts, n_e, rows_ge, sub), BF16),
            pltpu.VMEM((micros, parts, n_e, rows_ge, sub), BF16),
            dma((4,)), dma((3,)), dma((micros, parts)), dma((micros, parts)),
            dma((7,)), dma((micros, parts)), dma((micros, n_e - 1, parts)),
            dma((micros, n_e, n_a - 1, parts)), dma((micros, 2, n_a)), dma((micros, 2, n_a)),
            dma((micros, n_e, n_a - 1, parts)), dma((micros, parts)),
        ],
        compiler_params=pltpu.CompilerParams(
            collective_id=0, has_side_effects=True, vmem_limit_bytes=67043328
        ),
    )(tokens, gains, ids, weights, order, w_gate, w_up, w_down)


def solution(mesh):
    mesh_shape = (mesh.shape["pipe"], mesh.shape["tensor"], mesh.shape["expert"])
    return jax.shard_map(
        functools.partial(local, mesh_shape),
        mesh=mesh,
        in_specs=(
            P(None, "expert", None),
            P("pipe", None),
            P("pipe", None, "expert", None),
            P("pipe", None, "expert", None),
            P("pipe", None, "expert", None),
            P("pipe", "expert", None, "tensor"),
            P("pipe", "expert", None, "tensor"),
            P("pipe", "expert", "tensor", None),
        ),
        out_specs=P("pipe", None, "expert", "tensor"),
        check_vma=False,
    )
```

time: 98.7 us -> 85.4 us (0.87)
  Pallas kernels: 96.9 us -> 83.3 us
    pallas_call x1, Pallas kernels: 96.9 us -> 83.3 us  [local(): pl.pallas_call(functools.partial(layer_kernel, sizes), out_shape=jax.Shap...]
where the time goes in v1:
time: 85.4 us; the launch traced here: 85 us
  Pallas kernels  83.3 us (98%)
  local copies, waits for them, and re-layouts  1.67 us (2%)
    pallas_call x1, Pallas kernels, local(): pl.pallas_call(functools.partial(layer_kernel, sizes), out_shape=jax.Shap...  83.3 us

profile of v1, /device:TPU:6, one launch (start us, length us, event | category | flops | bytes accessed | tf_op | source)
XLA Modules:
  0.0 85.0 jit_solution(11319823702192224057)
XLA Ops:
  0.0 83.3 %shard_map.82 = bf16[1,2,64,1024]{3,2,1,0:T(8,128)(2,1)} custom-call(bf16[2,64,4096]{2,1,0:T(8,128)(2,1)} %tokens.1, f32[1,4096]{1,0:T(1,128)} %gains_in.1, s32[2,2,64]{2,1,0:T(2,128)} %bitcast.9, f32[2,2,64]{2,1,0:T(2,128)} %bitcast.10, s32[2,1,64]{2,1,0:T(1,128)} %bitcast.11, bf16[1,1,4096,384]{3,2,1,0:T(8,128)(2,1)} %w_gate.1, ...), custom_call_target="tpu_custom_call" | custom-call | tf_op jit(solution)/shard_map/pallas_call | solution.py:447
  83.3 1.7 %copy.11 = bf16[1,2,64,1024]{3,2,1,0:T(8,128)(2,1)} copy(bf16[1,2,64,1024]{3,2,1,0:T(8,128)(2,1)} %shard_map.82) | data formatting | bytes 524288

commit v2 on v1

--- a/solution.py
+++ b/solution.py
@@ -80,9 +80,6 @@
             for k in ks:
                 first_load(m, k).start()
 
-    for load in loads:
-        load.start()
-
     barrier = pltpu.get_barrier_semaphore()
 
     def greet(where):
@@ -148,6 +145,8 @@
 
     for load in small:
         load.wait()
+    for load in loads:
+        load.start()
     place(0)
 
     ends = jnp.where(p > 0, 1, 0) + jnp.where(p < n_p - 1, 1, 0)
@@ -211,21 +210,19 @@
             if d:
                 d_copy(m, d, k).start()
 
-    def forward(m, d):
-        for k in ks:
-            if d:
-                d_copy(m, d, k).wait_recv()
-            for da in range(1, n_a):
-                f_copy(m, d, da, k).start()
+    def forward(m, d, k):
+        if d:
+            d_copy(m, d, k).wait_recv()
+        for da in range(1, n_a):
+            f_copy(m, d, da, k).start()
+        if pair > 1:
+            c_copy(m, d, 0, k).start()
+
+    def pass_on(m, d, k):
+        for da in range(1, n_a):
+            f_copy(m, d, da, k).wait_recv()
             if pair > 1:
-                c_copy(m, d, 0, k).start()
-
-    def pass_on(m, d):
-        for k in ks:
-            for da in range(1, n_a):
-                f_copy(m, d, da, k).wait_recv()
-                if pair > 1:
-                    c_copy(m, d, da, k).start()
+                c_copy(m, d, da, k).start()
 
     squares = {}
 
@@ -251,18 +248,18 @@
             uq = u1 if uq is None else uq + u1
         squares[m, h] = ss
         if i == 0:
-            g_acc[...] = gq
-            u_acc[...] = uq
+            g_acc[h] = gq
+            u_acc[h] = uq
         else:
-            g_acc[...] += gq
-            u_acc[...] += uq
+            g_acc[h] += gq
+            u_acc[h] += uq
 
     def finish(m, h):
         if m == 0 and h == 0:
             loads[2].wait()
         inv = lax.rsqrt(squares[m, h] * (1.0 / (n_t * width)) + epsilon)
-        g = g_acc[...] * inv
-        hidden = (g / (1.0 + jnp.exp(-g)) * (u_acc[...] * inv)).astype(BF16)
+        g = g_acc[h] * inv
+        hidden = (g / (1.0 + jnp.exp(-g)) * (u_acc[h] * inv)).astype(BF16)
         order = list(range(1, n_a)) + [0]
         for dc in list(range(1, pair)) + [0]:
             for da in order:
@@ -291,33 +288,31 @@
                     if da:
                         y_copy(m, d, da, k).start()
 
-    def reduce_far(m, d):
-        for k in ks:
-            total = y_send[m, 0, d, k].astype(F32)
-            for da in range(1, n_a):
-                y_copy(m, d, da, k).wait_recv()
-                total = total + y_recv[m, da, d, k].astype(F32)
-            if d:
-                z_send[m, k, d] = total.astype(BF16)
-                z_copy(m, d, k).start()
-            else:
-                ret[m, k, z] = total.astype(BF16)
-
-    def combine(m):
-        for k in ks:
-            returned(m, k).wait_recv()
-            for d in range(n_e):
-                e = peer_e(d)
-                both = jnp.dot(comb[m, e], ret[m, k, e], preferred_element_type=F32)
-                g_part = both[:toks] + both[toks:]
-                update = g_part if d == 0 else update + g_part
-            fresh[m, k] = (h_in[m, k].astype(F32) + update).astype(BF16)
-
-            @pl.when(p < n_p - 1)
-            def _():
-                relay(m, k).start()
-
-            result(m, k).start()
+    def reduce_far(m, d, k):
+        total = y_send[m, 0, d, k].astype(F32)
+        for da in range(1, n_a):
+            y_copy(m, d, da, k).wait_recv()
+            total = total + y_recv[m, da, d, k].astype(F32)
+        if d:
+            z_send[m, k, d] = total.astype(BF16)
+            z_copy(m, d, k).start()
+        else:
+            ret[m, k, z] = total.astype(BF16)
+
+    def combine(m, k):
+        returned(m, k).wait_recv()
+        for d in range(n_e):
+            e = peer_e(d)
+            both = jnp.dot(comb[m, e], ret[m, k, e], preferred_element_type=F32)
+            g_part = both[:toks] + both[toks:]
+            update = g_part if d == 0 else update + g_part
+        fresh[m, k] = (h_in[m, k].astype(F32) + update).astype(BF16)
+
+        @pl.when(p < n_p - 1)
+        def _():
+            relay(m, k).start()
+
+        result(m, k).start()
 
     def step(fn, *args):
         return functools.partial(fn, *args)
@@ -325,73 +320,93 @@
     near, rest = halves[0], [d for d in halves[1] if d]
     last = len(ranks)
 
+    def gates(m, h, low, high):
+        return [step(gate, m, h, i) for i in range(low, high)]
+
+    def each(fn, m, blocks, parts_of=ks):
+        return [step(fn, m, d, k) for d in blocks for k in parts_of]
+
     def spread(m, first):
-        order = near + rest + [0]
-        if first:
-            steps = [step(arrive, m, k, first) for k in ks]
-            return steps + [step(dispatch, m, [(d, k) for d in order for k in ks])]
         steps = []
         for k in ks:
-            steps += [step(arrive, m, k, first), step(dispatch, m, [(d, k) for d in order])]
+            steps += [step(arrive, m, k, first), step(dispatch, m, [(d, k) for d in near])]
+        for k in ks:
+            steps += [step(dispatch, m, [(d, k) for d in rest])]
         return steps
 
-    def gates(m, h, low, high):
-        return [step(gate, m, h, i) for i in range(low, high)]
-
-    def each(fn, m, blocks):
-        return [step(fn, m, d) for d in blocks]
-
-    def plan_for(first):
-        plan = []
-        if not first:
-            plan += [step(place, m) for m in range(1, micros)]
-            plan += [step(weigh, m) for m in range(micros)]
-        plan += spread(0, first) + [step(forward, 0, 0)]
-        if first:
-            plan += [step(place, m) for m in range(1, micros)]
+    def keep(m):
+        return [step(dispatch, m, [(0, k) for k in ks])] + each(forward, m, [0])
+
+    early, late = list(ks)[:-1], list(ks)[-1:]
+
+    def body(m, ahead, between, held):
+        plan = each(forward, m, near) + gates(m, 0, 0, 1)
+        plan += each(forward, m, rest, early) + each(pass_on, m, near[:1], early)
+        plan += gates(m, 0, 1, pair) + ahead
+        plan += each(pass_on, m, [0]) + each(pass_on, m, near[:1], late) + each(pass_on, m, near[1:])
+        plan += gates(m, 0, pair, last - 1)
+        plan += each(forward, m, rest, late) + held + between
+        plan += gates(m, 1, 0, 1)
+        plan += gates(m, 0, last - 1, last)
+        plan += [step(finish, m, 0)]
+        plan += each(pass_on, m, rest, early)
+        plan += gates(m, 1, 1, pair)
+        plan += [step(reduce_pair, m, 0)]
+        plan += each(pass_on, m, rest, late)
+        plan += gates(m, 1, pair, last)
+        plan += [step(finish, m, 1)]
+        return plan
+
+    def joined(m):
+        return [step(combine, m, k) for k in ks]
+
+    def first_plan():
+        close = near[1:]
+        plan = spread(0, True) + keep(0)
+        for m in range(1, micros):
+            plan += [step(place, m)] + [step(arrive, m, k, True) for k in ks] + keep(m)
         for m in range(micros):
-            ahead = first and m
-            more = m + 1 < micros
-            plan += each(pass_on, m, [0])
-            if not ahead:
-                plan += each(forward, m, near)
-            plan += gates(m, 0, 0, pair)
-            if ahead:
-                plan += [step(combine, m - 1)]
-            plan += each(pass_on, m, near)
-            plan += gates(m, 0, pair, last - 1)
-            if not ahead:
-                plan += each(forward, m, rest)
-            if first and m == 0:
-                for n in range(1, micros):
-                    plan += spread(n, first)
-            plan += gates(m, 0, last - 1, last)
-            plan += [step(finish, m, 0)]
-            plan += gates(m, 1, 0, pair)
-            plan += [step(reduce_pair, m, 0)]
-            if m and not first:
-                plan += [step(combine, m - 1)]
-            plan += each(pass_on, m, rest)
-            plan += gates(m, 1, pair, last - 1)
-            if first:
-                plan += [step(weigh, m)]
-            plan += gates(m, 1, last - 1, last)
-            plan += [step(finish, m, 1)]
-            plan += each(reduce_far, m, near[:1])
+            more = range(m + 1, min(m + 2, micros))
+            far = [step(dispatch, n, [(d, k) for d in near[:1] + rest for k in ks]) for n in more]
+            side = [step(dispatch, n, [(d, k) for d in close for k in ks]) for n in more]
+            if m == 0:
+                moved = [go for n in more for go in each(forward, n, close)]
+                plan += side + body(m, far, moved, [])
+            else:
+                plan += gates(m, 0, 0, 1) + joined(m - 1)
+                plan += side + far + [go for n in more for go in each(forward, n, close)]
+                plan += each(pass_on, m, [0] + close) + gates(m, 0, 1, pair) + each(pass_on, m, near[:1])
+                plan += gates(m, 0, pair, last) + [step(finish, m, 0)]
+                plan += each(pass_on, m, rest, early) + gates(m, 1, 0, pair) + [step(reduce_pair, m, 0)]
+                plan += each(pass_on, m, rest, late) + gates(m, 1, pair, last) + [step(finish, m, 1)]
+            plan += [step(weigh, m)]
+            plan += each(reduce_far, m, near[:1], early) + [step(reduce_pair, m, 1)]
+            plan += each(reduce_far, m, near[:1], late)
+            for n in more:
+                plan += each(forward, n, near[:1])
+            plan += each(reduce_far, m, close)
+            for n in more:
+                plan += each(forward, n, rest)
+            plan += each(reduce_far, m, rest + [0])
+        return plan + joined(micros - 1)
+
+    def later_plan():
+        plan = [step(place, m) for m in range(1, micros)] + [step(weigh, m) for m in range(micros)]
+        for m in range(micros):
+            held = each(reduce_far, m - 1, near + rest + [0]) if m else []
+            plan += spread(m, False) + keep(m) + body(m, [], [], held)
+            if m + 1 == micros:
+                plan += each(reduce_far, m, near[:1], early)
             plan += [step(reduce_pair, m, 1)]
-            if more:
-                if first:
-                    plan += each(forward, m + 1, [0] + near + rest)
-                else:
-                    plan += spread(m + 1, first)
-                    plan += each(forward, m + 1, [0])
-            plan += each(reduce_far, m, near[1:] + rest + [0])
-        plan += [step(combine, micros - 1)]
-        return plan
+            if m:
+                plan += joined(m - 1)
+        plan += each(reduce_far, micros - 1, near[:1], late)
+        plan += each(reduce_far, micros - 1, near[1:] + rest + [0])
+        return plan + joined(micros - 1)
 
     def follow(first):
         squares.clear()
-        for go in plan_for(first):
+        for go in first_plan() if first else later_plan():
             go()
 
     @pl.when(p == 0)
@@ -463,8 +478,8 @@
             pltpu.VMEM(w_gate.shape[2:], BF16),
             pltpu.VMEM(w_up.shape[2:], BF16),
             pltpu.VMEM(w_down.shape[2:], BF16),
-            pltpu.VMEM((rows, hidden_width), F32),
-            pltpu.VMEM((rows, hidden_width), F32),
+            pltpu.VMEM((2, rows, hidden_width), F32),
+            pltpu.VMEM((2, rows, hidden_width), F32),
             pltpu.VMEM((micros, 2, n_a, parts, rows, sub), BF16),
             pltpu.VMEM((micros, 2, n_a, parts, rows, sub), BF16),
             pltpu.VMEM((micros, 2, n_a, parts, rows, sub), BF16),

time: 85.4 us -> 75.9 us (0.89)
  Pallas kernels: 83.3 us -> 73.8 us
    pallas_call x1, Pallas kernels: 83.3 us -> 73.8 us  [local(): pl.pallas_call(functools.partial(layer_kernel, sizes), out_shape=jax.Shap...]
where the time goes in v2:
time: 75.9 us; the launch traced here: 75.4 us
  Pallas kernels  73.8 us (97%)
  local copies, waits for them, and re-layouts  1.67 us (2%)
    pallas_call x1, Pallas kernels, local(): pl.pallas_call(functools.partial(layer_kernel, sizes), out_shape=jax.Shap...  73.8 us
    unnamed x1, local copies, waits for them, and re-layouts  1.67 us

profile of v2, /device:TPU:6, one launch (start us, length us, event | category | flops | bytes accessed | tf_op | source)
XLA Modules:
  0.0 75.4 jit_solution(5914238233892822903)
XLA Ops:
  0.0 73.8 %shard_map.82 = bf16[1,2,64,1024]{3,2,1,0:T(8,128)(2,1)} custom-call(bf16[2,64,4096]{2,1,0:T(8,128)(2,1)} %tokens.1, f32[1,4096]{1,0:T(1,128)} %gains_in.1, s32[2,2,64]{2,1,0:T(2,128)} %bitcast.9, f32[2,2,64]{2,1,0:T(2,128)} %bitcast.10, s32[2,1,64]{2,1,0:T(1,128)} %bitcast.11, bf16[1,1,4096,384]{3,2,1,0:T(8,128)(2,1)} %w_gate.1, ...), custom_call_target="tpu_custom_call" | custom-call | tf_op jit(solution)/shard_map/pallas_call | solution.py:462
  73.8 1.7 %copy.11 = bf16[1,2,64,1024]{3,2,1,0:T(8,128)(2,1)} copy(bf16[1,2,64,1024]{3,2,1,0:T(8,128)(2,1)} %shard_map.82) | data formatting | bytes 524288

commit v3 on v2

--- a/solution.py
+++ b/solution.py
@@ -17,7 +17,7 @@
     sizes, tokens, gains_in, ids_in, weights_in, picks_in, w_gate, w_up, w_down, out,
     gains, ids, weights, picks, placing, comb, h_in, fresh, send, x, wg, wu, wd, g_acc, u_acc, own, p_send, p_recv,
     y_send, y_recv, z_send, ret,
-    s_sem, w_sem, o_sem, h_loc, out_sem, h_recv, d_recv, f_recv, c_recv, p_sem, y_sem, z_sem,
+    s_sem, w_sem, h_loc, out_sem, h_recv, d_recv, f_recv, c_recv, p_sem, y_sem, z_sem,
 ):
     micros, n_p, n_t, n_e, pair, parts, rows_ge, width, capacity = sizes
     n_a = n_t // pair
@@ -59,11 +59,6 @@
     def first_load(m, k):
         cols = pl.ds(pl.multiple_of(r * width + k * sub, sub), sub)
         return pltpu.make_async_copy(tokens.at[m, :, cols], h_in.at[m, k], h_loc.at[m, k])
-
-    def result(m, k):
-        return pltpu.make_async_copy(
-            fresh.at[m, k], out.at[0, m, :, k * sub:(k + 1) * sub], o_sem.at[m, k]
-        )
 
     small = [
         pltpu.make_async_copy(src, dst, s_sem.at[i])
@@ -312,7 +307,7 @@
         def _():
             relay(m, k).start()
 
-        result(m, k).start()
+        out[0, m, :, k * sub:(k + 1) * sub] = fresh[m, k]
 
     def step(fn, *args):
         return functools.partial(fn, *args)
@@ -428,10 +423,6 @@
         sent(x.at[:, 0:n_a], 3)
         sent(p_send, 4)
     sent(z_send.at[:, :, 1:n_e], 6)
-    for m in range(micros):
-        for k in ks:
-            result(m, k).wait()
-
     @pl.when(p < n_p - 1)
     def _():
         sent(fresh, 0)
@@ -461,9 +452,9 @@
     pinned = pl.BlockSpec(memory_space=pl.ANY)
     return pl.pallas_call(
         functools.partial(layer_kernel, sizes),
-        out_shape=jax.ShapeDtypeStruct((1, micros, toks, width), BF16),
+        out_shape=pltpu.VMEM((1, micros, toks, width), BF16),
         in_specs=[pinned] * 8,
-        out_specs=pinned,
+        out_specs=pl.BlockSpec(memory_space=pltpu.VMEM),
         scratch_shapes=[
             pltpu.VMEM(gains.shape, F32),
             pltpu.VMEM(ids.shape, jnp.int32),
@@ -487,13 +478,13 @@
             pltpu.VMEM((micros, n_a, n_e, parts, rows_ge, sub), BF16),
             pltpu.VMEM((micros, parts, n_e, rows_ge, sub), BF16),
             pltpu.VMEM((micros, parts, n_e, rows_ge, sub), BF16),
-            dma((4,)), dma((3,)), dma((micros, parts)), dma((micros, parts)),
+            dma((4,)), dma((3,)), dma((micros, parts)),
             dma((7,)), dma((micros, parts)), dma((micros, n_e - 1, parts)),
             dma((micros, n_e, n_a - 1, parts)), dma((micros, 2, n_a)), dma((micros, 2, n_a)),
             dma((micros, n_e, n_a - 1, parts)), dma((micros, parts)),
         ],
         compiler_params=pltpu.CompilerParams(
-            collective_id=0, has_side_effects=True, vmem_limit_bytes=67043328
+            collective_id=0, has_side_effects=True, vmem_limit_bytes=66584576
         ),
     )(tokens, gains, ids, weights, order, w_gate, w_up, w_down)
 

time: 75.9 us -> 74.3 us (0.979)
  local copies, waits for them, and re-layouts: 1.67 us -> 0.71 us
    unnamed x1, local copies, waits for them, and re-layouts: 1.67 us -> 0.71 us
where the time goes in v3:
time: 74.3 us; the launch traced here: 73.8 us
  Pallas kernels  73.1 us (98%)
    pallas_call x1, Pallas kernels, local(): pl.pallas_call(functools.partial(layer_kernel, sizes), out_shape=pltpu.VM...  73.1 us

profile of v3, /device:TPU:6, one launch (start us, length us, event | category | flops | bytes accessed | tf_op | source)
XLA Modules:
  0.0 73.8 jit_solution(6993080361538009332)
XLA Ops:
  0.0 73.1 %shard_map.82 = bf16[1,2,64,1024]{3,2,1,0:T(8,128)(2,1)S(1)} custom-call(bf16[2,64,4096]{2,1,0:T(8,128)(2,1)} %tokens.1, f32[1,4096]{1,0:T(1,128)} %gains_in.1, s32[2,2,64]{2,1,0:T(2,128)} %bitcast.9, f32[2,2,64]{2,1,0:T(2,128)} %bitcast.10, s32[2,1,64]{2,1,0:T(1,128)} %bitcast.11, bf16[1,1,4096,384]{3,2,1,0:T(8,128)(2,1)} %w_gate.1, ...), custom_call_target="tpu_custom_call" | custom-call | tf_op jit(solution)/shard_map/pallas_call | solution.py:453
  73.1 0.7 copy.11
